TPU v7x, 256 devices: a whole 4x4x8 slice. The times are simulated.
256 devices in a mesh: bank: 64 (over z, y, x_lo), ens: 4 (over x_hi, core).
Axes of the slice: x: 4 (x_hi: 2, x_lo: 2; x = x_hi * 2 + x_lo), y: 4, z: 8, core: 2. Of those that a mesh axis runs over, the one named last changes fastest.
Arguments:
- item_ids: int32 [8192, 2], P(('ens', 'bank')), parts along dimension 0, may hold values from 0 to 16383
- large_table: bfloat16 [65536, 256], P(('ens', 'bank')), parts along dimension 0, may hold values from -6 to 6
- dense_part: float32 [8192, 256], P(('ens', 'bank')), parts along dimension 0, may hold values from -6 to 6
- small_ids: int32 [8192], P(('ens', 'bank')), parts along dimension 0, may hold values from 0 to 127
- small_table: bfloat16 [512, 256], P(('ens', 'bank')), parts along dimension 0, may hold values from -6 to 6
- scale_ids: int32 [8192], P(('ens', 'bank')), parts along dimension 0, may hold values from 0 to 127
Outputs:
- features: float32 [8192, 256], P(('ens', 'bank')), parts along dimension 0
There are 4 independent parts, one for each index of `ens`. A program takes and returns all parts, laid end to end along the dimension named above; each array names one. Nothing has to cross between parts.
All inputs are finite; a program needn't handle non-finite values.
Results may differ from a plain program's by a relative error of at most 0.0003.
Values may be sent and summed in bfloat16 or wider, within the bound.
A program may use at most 64 MiB of HBM per device.

v0:
```python
import jax
import jax.numpy as jnp
from jax import lax
from jax.sharding import PartitionSpec as P

PICKS = 2


def laid_out(blocks, dim):
    lengths = list(blocks.shape[1:])
    lengths[dim] *= blocks.shape[0]
    return jnp.moveaxis(blocks, 0, dim).reshape(lengths)


def from_everyone(value, axis):
    length = lax.axis_size(axis)
    return lax.all_to_all(
        jnp.broadcast_to(value[None], (length, *value.shape)), axis, 0, 0, tiled=True
    )


def collect(value, axis, dim):
    return laid_out(from_everyone(value, axis), dim)


def in_blocks(value, dim, length):
    lengths = value.shape
    blocks = value.reshape(*lengths[:dim], length, lengths[dim] // length, *lengths[dim + 1 :])
    return jnp.moveaxis(blocks, dim, 0)


def sum_at_owner(value, axis, dim):
    blocks = in_blocks(value, dim, lax.axis_size(axis))
    arrived = lax.all_to_all(blocks, axis, split_axis=0, concat_axis=0, tiled=True)
    return arrived.sum(axis=0)


def local_rows(table_part, wanted, first_row):
    place = wanted - first_row
    inside = (place >= 0) & (place < table_part.shape[0])
    found = jnp.take(table_part, jnp.clip(place, 0, table_part.shape[0] - 1), axis=0).astype(
        jnp.float32
    )
    return jnp.where(inside[..., None], found, 0.0)


def shards(item_ids, large_table, dense_part, small_ids, small_table, scale_ids):
    big_first = lax.axis_index("bank") * large_table.shape[0]
    all_ids = collect(item_ids, "bank", 0)
    pooled = sum_at_owner(
        jnp.sum(local_rows(large_table, all_ids, big_first), axis=1), "bank", 0
    ) * PICKS ** (-0.5)
    every_row = collect(small_table, "bank", 0)
    small_rows = jnp.take(every_row, small_ids, axis=0).astype(jnp.float32)
    scale_rows = jnp.take(every_row, scale_ids, axis=0).astype(jnp.float32)
    dense_part = dense_part * scale_rows
    total = dense_part + pooled * small_rows
    power = jnp.mean(total * total, axis=-1, keepdims=True)
    features = total * lax.rsqrt(power + 1e-06)
    return features


def solution(mesh):
    return jax.shard_map(
        shards,
        mesh=mesh,
        in_specs=(
            P(("ens", "bank"), None),
            P(("ens", "bank"), None),
            P(("ens", "bank"), None),
            P(("ens", "bank")),
            P(("ens", "bank"), None),
            P(("ens", "bank")),
        ),
        out_specs=P(("ens", "bank"), None),
        check_vma=False,
    )
```

profile of v0, /device:TPU:2, one launch (start us, length us, event | category | flops | bytes accessed | tf_op | source)
XLA Modules:
  0.0 126.0 jit_solution(9171903706651911703)
XLA Ops:
  0.0 0.0 copy-start
  0.0 1.3 %broadcast_in_dim.46 = s32[64,32,2]{1,2,0:T(2,128)} broadcast(s32[32,2]{0,1:T(2,128)} %param.8), dimensions={1,2} | broadcast | bytes 16640 | tf_op jit(solution)/shard_map/broadcast_in_dim | solution.py:18
  1.4 13.1 %all-to-all-start.1 = ((s32[64,32,2]{1,2,0:T(2,128)}), s32[64,32,2]{1,2,0:T(2,128)S(1)}, u32[]{:S(2)}, u32[]{:S(2)}) async-start(s32[64,32,2]{1,2,0:T(2,128)} %broadcast_in_dim.46), calls=%async_computation.1 | async-start | bytes 131072 | tf_op jit(solution)/shard_map/all_to_all | solution.py:17
  14.5 9.8 %all-to-all-done.1 = s32[64,32,2]{1,2,0:T(2,128)S(1)} async-done(((s32[64,32,2]{1,2,0:T(2,128)}), s32[64,32,2]{1,2,0:T(2,128)S(1)}, u32[]{:S(2)}, u32[]{:S(2)}) %all-to-all-start.1) | async-done | bytes 16416 | tf_op jit(solution)/shard_map/all_to_all | solution.py:17
  24.3 1.3 %broadcast_in_dim.45 = bf16[64,2,256]{2,1,0:T(2,128)(2,1)} broadcast(bf16[2,256]{1,0:T(2,128)(2,1)} %param.12), dimensions={1,2} | broadcast | bytes 66560 | tf_op jit(solution)/shard_map/broadcast_in_dim | solution.py:18
  25.6 5.4 %all-to-all-start = ((bf16[64,2,256]{2,1,0:T(2,128)(2,1)}), bf16[64,2,256]{2,1,0:T(2,128)(2,1)S(1)}, u32[]{:S(2)}, u32[]{:S(2)}) async-start(bf16[64,2,256]{2,1,0:T(2,128)(2,1)} %broadcast_in_dim.45), calls=%async_computation | async-start | bytes 131072 | tf_op jit(solution)/shard_map/all_to_all | solution.py:17
  31.0 0.1 copy.21
  31.1 0.1 copy.24
  31.2 0.1 min.18
  31.3 0.1 min.16
  31.4 0.4 copy.27
  31.8 0.5 reshape.91
  32.3 0.0 copy-done
  32.3 14.6 %gather_fusion = bf16[4096,256]{1,0:T(8,128)(2,1)S(1)} fusion(bf16[256,256]{1,0:T(8,128)(2,1)S(1)} %copy-done, s32[4096]{0:T(1024)S(1)} %broadcast_clamp_fusion), kind=kCustom, calls=%fused_computation.2 | custom fusion | bytes 4210688 | tf_op jit(solution)/shard_map/jit(_take)/gather | solution.py:41
  46.9 2.2 %reshape.90 = bf16[2048,2,256]{2,1,0:T(2,128)(2,1)} reshape(bf16[4096,256]{1,0:T(8,128)(2,1)S(1)} %gather_fusion) | data formatting | bytes 4194304 | tf_op jit(solution)/shard_map/jit(_take)/gather | solution.py:41
  49.2 0.5 copy.25
  49.6 1.0 copy.28
  50.6 14.2 %select_reduce_fusion = f32[2048,256]{1,0:T(8,128)} fusion(pred[2048,2]{1,0:T(8,128)(4,1)S(1)} %bitcast.8, bf16[2048,2,256]{2,1,0:T(2,128)(2,1)} %reshape.90, pred[2048,2]{1,0:T(8,128)(4,1)S(1)} %copy.25), kind=kLoop, calls=%fused_computation.3 | loop fusion | flops 3670016 | bytes 4202496 | tf_op jit(solution)/shard_map/reduce_sum | solution.py:51
  64.8 0.0 all-to-all-done
  64.9 0.0 copy-start.3
  64.9 0.0 copy-start.2
  64.9 11.4 %all-to-all-start.2 = ((f32[64,32,256]{2,1,0:T(8,128)}), f32[64,32,256]{2,1,0:T(8,128)S(1)}, u32[]{:S(2)}, u32[]{:S(2)}) async-start(f32[64,32,256]{2,1,0:T(8,128)} %bitcast.1), calls=%async_computation.2 | async-start | bytes 4194304 | tf_op jit(solution)/shard_map/all_to_all | solution.py:34
  76.3 0.0 copy-done.3
  76.3 0.0 copy-start.1
  76.4 0.0 copy-done.2
  76.4 0.6 gather_fusion.1
  77.1 0.6 gather_fusion.2
  77.7 47.3 %all-to-all-done.2 = f32[64,32,256]{2,1,0:T(8,128)S(1)} async-done(((f32[64,32,256]{2,1,0:T(8,128)}), f32[64,32,256]{2,1,0:T(8,128)S(1)}, u32[]{:S(2)}, u32[]{:S(2)}) %all-to-all-start.2) | async-done | bytes 2097184 | tf_op jit(solution)/shard_map/all_to_all | solution.py:34
  125.0 0.1 reduce_sum.28
  125.1 0.0 copy-done.1
  125.1 0.2 multiply_reduce_fusion
  125.3 0.7 broadcast_multiply_fusion
  (12 shorter events, 0.1 us)
Async XLA Ops:
  0.0 32.3 %copy-start = (bf16[256,256]{1,0:T(8,128)(2,1)S(1)}, bf16[256,256]{1,0:T(8,128)(2,1)}, u32[]{:S(2)}) copy-start(bf16[256,256]{1,0:T(8,128)(2,1)} %param.9) | copy-start | bytes 393220
  1.4 22.9 %all-to-all-start.1 = ((s32[64,32,2]{1,2,0:T(2,128)}), s32[64,32,2]{1,2,0:T(2,128)S(1)}, u32[]{:S(2)}, u32[]{:S(2)}) async-start(s32[64,32,2]{1,2,0:T(2,128)} %broadcast_in_dim.46), calls=%async_computation.1 | async-start | bytes 131072 | tf_op jit(solution)/shard_map/all_to_all | solution.py:17
  25.6 39.2 %all-to-all-start = ((bf16[64,2,256]{2,1,0:T(2,128)(2,1)}), bf16[64,2,256]{2,1,0:T(2,128)(2,1)S(1)}, u32[]{:S(2)}, u32[]{:S(2)}) async-start(bf16[64,2,256]{2,1,0:T(2,128)(2,1)} %broadcast_in_dim.45), calls=%async_computation | async-start | bytes 131072 | tf_op jit(solution)/shard_map/all_to_all | solution.py:17
  64.9 11.5 %copy-start.3 = (s32[32]{0:T(128)S(1)}, s32[32]{0:T(128)}, u32[]{:S(2)}) copy-start(s32[32]{0:T(128)} %param.13) | copy-start | bytes 388
  64.9 11.5 %copy-start.2 = (s32[32]{0:T(128)S(1)}, s32[32]{0:T(128)}, u32[]{:S(2)}) copy-start(s32[32]{0:T(128)} %param.11) | copy-start | bytes 388
  64.9 60.1 %all-to-all-start.2 = ((f32[64,32,256]{2,1,0:T(8,128)}), f32[64,32,256]{2,1,0:T(8,128)S(1)}, u32[]{:S(2)}, u32[]{:S(2)}) async-start(f32[64,32,256]{2,1,0:T(8,128)} %bitcast.1), calls=%async_computation.2 | async-start | bytes 4194304 | tf_op jit(solution)/shard_map/all_to_all | solution.py:34
  76.3 48.8 %copy-start.1 = (f32[32,256]{1,0:T(8,128)S(1)}, f32[32,256]{1,0:T(8,128)}, u32[]{:S(2)}) copy-start(f32[32,256]{1,0:T(8,128)} %param.10) | copy-start | bytes 98308
where the time goes:
time: 127 us; the launch traced here: 126 us
  waiting for transfers between devices  57.1 us (45%)
  starting transfers between devices  29.9 us (24%)
  local copies, waits for them, and re-layouts  23.4 us (18%)
  other arithmetic  15.4 us (12%)
    all_to_all x1, waiting for transfers between devices, sum_at_owner(): lax.all_to_all(blocks, axis, split_axis=0, concat_axis=0, tiled=True)  47.3 us
    all_to_all x2, starting transfers between devices, from_everyone(): lax.all_to_all(jnp.broadcast_to(value[None], (length, *value.shape)), axi...  18.5 us
    gather x2, local copies, waits for them, and re-layouts, local_rows(): jnp.take(table_part, jnp.clip(place, 0, table_part.shape[0] - 1), axis=0)  16.8 us
    reduce_sum x1, other arithmetic, shards(): jnp.sum(local_rows(large_table, all_ids, big_first), axis=1)  14.2 us
    all_to_all x1, starting transfers between devices, sum_at_owner(): lax.all_to_all(blocks, axis, split_axis=0, concat_axis=0, tiled=True)  11.4 us
    all_to_all x2, waiting for transfers between devices, from_everyone(): lax.all_to_all(jnp.broadcast_to(value[None], (length, *value.shape)), axi...  9.82 us
    broadcast_in_dim x2, local copies, waits for them, and re-layouts, from_everyone(): jnp.broadcast_to(value[None], (length, *value.shape))  2.67 us
  transfers between devices with their start and end apart: 3, of which 2 were waited for; matrix products, arithmetic and copies ran while one was open for 28% of the time, Pallas kernels for 0%

commit v1 on v0

v1 whole, which is shorter than its diff:
```python
import jax
import jax.numpy as jnp
from jax import lax
from jax.experimental import pallas as pl
from jax.experimental.pallas import tpu as pltpu
from jax.sharding import PartitionSpec as P

PICKS = 2
NZ, NY, NX = 8, 4, 2
Z_ORDER = (4, 3, 5, 2, 6, 1, 7)
MESH = pl.DeviceIdType.MESH


def kernel(
    ids_hbm,
    table_hbm,
    dense_hbm,
    small_ids_hbm,
    scale_ids_hbm,
    small_hbm,
    out_ref,
    tab,
    idb,
    smb,
    dense,
    picks,
    onehot,
    part,
    x_out,
    x_in,
    z_out,
    z_in,
    local_sem,
    y_send,
    y_recv,
    r_send,
    r_recv,
    ids_send,
    ids_recv,
    sm_send,
    sm_recv,
    xx_send,
    xx_recv,
    zz_send,
    zz_recv,
):
    bank = lax.axis_index("bank")
    x = lax.rem(bank, NX)
    y = lax.rem(bank // NX, NY)
    z = bank // (NX * NY)

    def at(dz, dy, flip):
        zz = lax.rem(z + dz, NZ)
        yy = lax.rem(y + dy, NY)
        xx = 1 - x if flip else x
        return (zz * NY + yy) * NX + xx

    def remote(src, dst, send, recv, to):
        return pltpu.make_async_remote_copy(
            src_ref=src,
            dst_ref=dst,
            send_sem=send,
            recv_sem=recv,
            device_id={"bank": to},
            device_id_type=MESH,
        )

    rows = table_hbm.shape[0]
    half = rows // 2
    peers_z = [at(k, 0, False) for k in range(NZ)]
    peers_y = [at(0, k, False) for k in range(NY)]
    peer_x = at(0, 0, True)

    barrier = pltpu.get_barrier_semaphore()
    for to in [peer_x] + peers_y[1:] + peers_z[1:]:
        pl.semaphore_signal(barrier, inc=1, device_id={"bank": to}, device_id_type=MESH)

    loads = [
        pltpu.make_async_copy(table_hbm.at[:, pl.ds(0, 128)], tab.at[0, 0], local_sem.at[0]),
        pltpu.make_async_copy(table_hbm.at[:, pl.ds(128, 128)], tab.at[0, 1], local_sem.at[1]),
        pltpu.make_async_copy(ids_hbm, idb.at[0, 0], local_sem.at[2]),
        pltpu.make_async_copy(small_hbm, smb.at[0, 0, 0], local_sem.at[3]),
        pltpu.make_async_copy(dense_hbm, dense, local_sem.at[4]),
        pltpu.make_async_copy(small_ids_hbm, picks.at[0], local_sem.at[5]),
        pltpu.make_async_copy(scale_ids_hbm, picks.at[1], local_sem.at[6]),
    ]
    for load in loads:
        load.start()
    for load in loads:
        load.wait()
    pl.semaphore_wait(barrier, 1 + (NY - 1) + (NZ - 1))

    sent = []

    def go(copy):
        copy.start()
        sent.append(copy)
        return copy

    ids_x = go(remote(idb.at[0, 0], idb.at[0, 1], ids_send.at[0], ids_recv.at[0], peer_x))
    sm_x = go(remote(smb.at[0, 0, 0], smb.at[0, 0, 1], sm_send.at[0], sm_recv.at[0], peer_x))

    own = {}
    for h in range(2):
        for up, r in ((0, 0), (1, 1), (0, 1), (1, 0)):
            slot, to = (3, peers_y[1]) if up == 0 else (1, peers_y[3])
            piece = pl.ds(r * half, half)
            own[up, h, r] = go(
                remote(
                    tab.at[0, h, piece],
                    tab.at[slot, h, piece],
                    y_send.at[up, h, r],
                    y_recv.at[up, h, r],
                    to,
                )
            )

    ids_x.wait_recv()
    ids_z = [
        go(remote(idb.at[0], idb.at[(NZ - k) % NZ], ids_send.at[k], ids_recv.at[k], peers_z[k]))
        for k in Z_ORDER
    ]
    sm_x.wait_recv()
    sm_z = [
        go(
            remote(
                smb.at[0, 0], smb.at[0, (NZ - k) % NZ], sm_send.at[k], sm_recv.at[k], peers_z[k]
            )
        )
        for k in Z_ORDER
    ]

    relay = {}
    for h in range(2):
        for up in range(2):
            slot, to = (3, peers_y[1]) if up == 0 else (1, peers_y[3])
            own[up, h, up].wait_recv()
            piece = pl.ds(up * half, half)
            relay[up, h] = go(
                remote(
                    tab.at[slot, h, piece],
                    tab.at[2, h, piece],
                    r_send.at[up, h],
                    r_recv.at[up, h],
                    to,
                )
            )

    for copy in ids_z:
        copy.wait_recv()
    examples = idb.shape[-1]
    cols = idb[...].reshape(NZ * NX * PICKS, examples).T
    lane = lax.broadcasted_iota(jnp.int32, (examples, rows), 1)
    for kx in range(NX):
        for kz in range(NZ):
            c = (kz * NX + kx) * PICKS
            d = kx * NZ + kz
            for ky in range(NY):
                base = peers_y[ky] * rows
                first = (cols[:, c : c + 1] - base) == lane
                second = (cols[:, c + 1 : c + 2] - base) == lane
                count = jnp.where(first, 1.0, 0.0) + jnp.where(second, 1.0, 0.0)
                onehot[d * examples : (d + 1) * examples, ky * rows : (ky + 1) * rows] = (
                    count.astype(jnp.bfloat16)
                )

    for copy in sm_z:
        copy.wait_recv()
    sm_y = [
        go(
            remote(
                smb.at[0], smb.at[(NY - k) % NY], sm_send.at[NZ + k], sm_recv.at[NZ + k], peers_y[k]
            )
        )
        for k in (2, 1, 3)
    ]

    block = NZ * examples

    def partial(kx, h):
        total = None
        for ky in (0, 1, 3, 2):
            term = jnp.dot(
                onehot[kx * block : (kx + 1) * block, ky * rows : (ky + 1) * rows],
                tab[ky, h],
                preferred_element_type=jnp.float32,
            )
            total = term if total is None else total + term
        return total.reshape(NZ, examples, 128)

    swap = {}
    for h in range(2):
        own[0, h, 1].wait_recv()
        own[1, h, 0].wait_recv()
        relay[0, h].wait_recv()
        relay[1, h].wait_recv()
        x_out[h] = partial(1, h)
        for k in Z_ORDER + (0,):
            swap[k, h] = go(
                remote(
                    x_out.at[h, k], x_in.at[h, k], xx_send.at[h, k], xx_recv.at[h, k], peer_x
                )
            )
        part[h] = partial(0, h)

    deliver = []
    for h in range(2):
        for k in Z_ORDER:
            swap[k, h].wait_recv()
            z_out[h, k] = part[h, k] + x_in[h, k]
            deliver.append(
                go(
                    remote(
                        z_out.at[h, k],
                        z_in.at[h, (NZ - k) % NZ],
                        zz_send.at[h, k],
                        zz_recv.at[h, k],
                        peers_z[k],
                    )
                )
            )
    for h in range(2):
        swap[0, h].wait_recv()

    for copy in sm_y:
        copy.wait_recv()
    small = smb[...].reshape(NY * NZ * NX * 2, 256)
    place = lax.broadcasted_iota(jnp.int32, (examples, NY * NZ * NX * 2), 1)
    sx = lax.rem(place // 2 + x, NX)
    sz = lax.rem(place // (2 * NX) + z, NZ)
    sy = lax.rem(place // (2 * NX * NZ) + y, NY)
    row = ((sz * NY + sy) * NX + sx) * 2 + lax.rem(place, 2)
    pick_cols = picks[...].reshape(2, examples).T
    found = [
        jnp.dot(
            jnp.where(pick_cols[:, i : i + 1] == row, 1.0, 0.0).astype(jnp.bfloat16),
            small,
            preferred_element_type=jnp.float32,
        )
        for i in range(2)
    ]
    scaled = dense[...] * found[1]

    for copy in deliver:
        copy.wait_recv()
    totals = []
    for h in range(2):
        pooled = part[h, 0] + x_in[h, 0]
        for k in range(1, NZ):
            pooled += z_in[h, k]
        pooled = pooled * PICKS ** (-0.5)
        cut = slice(h * 128, (h + 1) * 128)
        totals.append(scaled[:, cut] + pooled * found[0][:, cut])
    power = (
        jnp.sum(totals[0] * totals[0] + totals[1] * totals[1], axis=-1, keepdims=True) / 256.0
    )
    inv = lax.rsqrt(power + 1e-06)
    for h in range(2):
        out_ref[:, h * 128 : (h + 1) * 128] = totals[h] * inv

    for copy in sent:
        copy.wait_send()


def shards(item_ids, large_table, dense_part, small_ids, small_table, scale_ids):
    examples, features = dense_part.shape
    rows = large_table.shape[0]
    any_space = pl.BlockSpec(memory_space=pl.ANY)
    dma = pltpu.SemaphoreType.DMA
    return pl.pallas_call(
        kernel,
        out_shape=jax.ShapeDtypeStruct((examples, features), jnp.float32),
        in_specs=[any_space] * 6,
        out_specs=pl.BlockSpec(memory_space=pltpu.VMEM),
        scratch_shapes=[
            pltpu.VMEM((NY, 2, rows, 128), jnp.bfloat16),
            pltpu.VMEM((NZ, NX, PICKS, examples), jnp.int32),
            pltpu.VMEM((NY, NZ, NX, 2, features), jnp.bfloat16),
            pltpu.VMEM((examples, features), jnp.float32),
            pltpu.VMEM((2, 1, examples), jnp.int32),
            pltpu.VMEM((NX * NZ * examples, NY * rows), jnp.bfloat16),
            pltpu.VMEM((2, NZ, examples, 128), jnp.float32),
            pltpu.VMEM((2, NZ, examples, 128), jnp.float32),
            pltpu.VMEM((2, NZ, examples, 128), jnp.float32),
            pltpu.VMEM((2, NZ, examples, 128), jnp.float32),
            pltpu.VMEM((2, NZ, examples, 128), jnp.float32),
            dma((7,)),
            dma((2, 2, 2)),
            dma((2, 2, 2)),
            dma((2, 2)),
            dma((2, 2)),
            dma((NZ,)),
            dma((NZ,)),
            dma((NZ + NY,)),
            dma((NZ + NY,)),
            dma((2, NZ)),
            dma((2, NZ)),
            dma((2, NZ)),
            dma((2, NZ)),
        ],
        compiler_params=pltpu.CompilerParams(collective_id=0, has_side_effects=True),
    )(
        item_ids.T,
        large_table,
        dense_part,
        small_ids.reshape(1, examples),
        scale_ids.reshape(1, examples),
        small_table,
    )


def solution(mesh):
    return jax.shard_map(
        shards,
        mesh=mesh,
        in_specs=(
            P(("ens", "bank"), None),
            P(("ens", "bank"), None),
            P(("ens", "bank"), None),
            P(("ens", "bank")),
            P(("ens", "bank"), None),
            P(("ens", "bank")),
        ),
        out_specs=P(("ens", "bank"), None),
        check_vma=False,
    )
```

time: 127 us -> 28.6 us (0.23)
  the two profiles are of different devices: /device:TPU:2 before, /device:TPU:26 now
where the time goes in v1:
time: 28.6 us; the launch traced here: 28.4 us
  Pallas kernels  27.1 us (95%)
  local copies, waits for them, and re-layouts  1.38 us (5%)
    pallas_call x1, Pallas kernels, shards(): pl.pallas_call(kernel, out_shape=jax.ShapeDtypeStruct((examples, features...  27.1 us
    unnamed x1, local copies, waits for them, and re-layouts  1.38 us

profile of v1, /device:TPU:26, one launch (start us, length us, event | category | flops | bytes accessed | tf_op | source)
XLA Modules:
  0.0 28.4 jit_solution(1464977216679066119)
XLA Ops:
  0.0 27.1 %shard_map.64 = f32[32,256]{1,0:T(8,128)} custom-call(s32[2,32]{1,0:T(2,128)} %bitcast.3, bf16[256,256]{1,0:T(8,128)(2,1)} %table_hbm.1, f32[32,256]{1,0:T(8,128)} %dense_hbm.1, s32[1,32]{1,0:T(1,128)} %bitcast.4, s32[1,32]{1,0:T(1,128)} %bitcast.5, bf16[2,256]{1,0:T(2,128)(2,1)} %small_hbm.1), custom_call_target="tpu_custom_call" | custom-call | tf_op jit(solution)/shard_map/pallas_call | solution.py:270
  27.1 1.4 %copy.8 = f32[32,256]{1,0:T(8,128)} copy(f32[32,256]{1,0:T(8,128)} %shard_map.64) | data formatting | bytes 65536

commit v2 on v0

v2 whole, which is shorter than its diff:
```python
import jax
import jax.numpy as jnp
from jax import lax
from jax.experimental import pallas as pl
from jax.experimental.pallas import tpu as pltpu
from jax.sharding import PartitionSpec as P

PICKS = 2
NZ, NY, NX = 8, 4, 2
FAR_FIRST = (4, 3, 5, 2, 6, 1, 7, 0)
MESH = pl.DeviceIdType.MESH


def kernel(
    ids_hbm,
    table_hbm,
    dense_hbm,
    small_ids_hbm,
    scale_ids_hbm,
    small_hbm,
    out_ref,
    tab,
    idb,
    smb,
    dense,
    picks,
    onehot,
    part,
    x_out,
    x_in,
    z_out,
    z_in,
    load_sem,
    send_sem,
    recv_sem,
    x_sem,
    up_sem,
    y_sem,
):
    bank = lax.axis_index("bank")
    x = lax.rem(bank, NX)
    y = lax.rem(bank // NX, NY)
    z = bank // (NX * NY)

    def at(dz, dy, flip):
        zz = lax.rem(z + dz, NZ)
        yy = lax.rem(y + dy, NY)
        xx = 1 - x if flip else x
        return (zz * NY + yy) * NX + xx

    def remote(src, dst, send, recv, to):
        return pltpu.make_async_remote_copy(
            src_ref=src,
            dst_ref=dst,
            send_sem=send,
            recv_sem=recv,
            device_id={"bank": to},
            device_id_type=MESH,
        )

    rows = table_hbm.shape[0]
    examples = dense_hbm.shape[0]
    column = [(k, 1) for k in FAR_FIRST] + [(k, 0) for k in FAR_FIRST]
    slot_at = [column.index((-k % NZ, flip)) for k, flip in column]
    others = NX * NZ - 1
    peers_y = [at(0, k, 0) for k in range(NY)]

    barrier = pltpu.get_barrier_semaphore()
    for to in peers_y[1:] + [at(k, 0, flip) for k, flip in column[:-1]]:
        pl.semaphore_signal(barrier, inc=1, device_id={"bank": to}, device_id_type=MESH)

    loads = [
        pltpu.make_async_copy(table_hbm.at[:, pl.ds(0, 128)], tab.at[0, 0], load_sem.at[0]),
        pltpu.make_async_copy(table_hbm.at[:, pl.ds(128, 128)], tab.at[1, 0], load_sem.at[6]),
        pltpu.make_async_copy(ids_hbm, idb.at[others], load_sem.at[1]),
        pltpu.make_async_copy(small_hbm, smb.at[0, others], load_sem.at[2]),
        pltpu.make_async_copy(dense_hbm, dense, load_sem.at[3]),
        pltpu.make_async_copy(small_ids_hbm, picks.at[0], load_sem.at[4]),
        pltpu.make_async_copy(scale_ids_hbm, picks.at[1], load_sem.at[5]),
    ]
    for load in loads:
        load.start()
    for load in loads:
        load.wait()
    pl.semaphore_wait(barrier, NY - 1 + others)

    half = rows // 2
    towards = ((peers_y[1], NY - 1), (peers_y[NY - 1], 1))
    def to_neighbour(up, relayed):
        to, slot = towards[up]
        piece = pl.ds((up if relayed else 1 - up) * half, half)
        remote(
            tab.at[1, 0, piece],
            tab.at[1, slot, piece],
            send_sem.at[0],
            up_sem.at[up] if relayed else y_sem.at[1],
            to,
        ).start()

    for up in range(2):
        to_neighbour(up, True)
    for k in (1, 3, 2):
        remote(tab.at[0, 0], tab.at[0, NY - k], send_sem.at[0], y_sem.at[0], peers_y[k]).start()
    for up in range(2):
        to_neighbour(up, False)
    for buf, i in ((idb, 1), (smb.at[0], 2)):
        for (k, flip), slot in zip(column[:-1], slot_at):
            remote(
                buf.at[others], buf.at[slot], send_sem.at[i], recv_sem.at[i], at(k, 0, flip)
            ).start()

    def all_of(ref, send, recv):
        return remote(ref, ref, send, recv, peers_y[1])

    for up in range(2):
        to, slot = towards[up]
        piece = pl.ds(up * half, half)
        all_of(tab.at[1, slot, piece], send_sem.at[0], up_sem.at[up]).wait_recv()
        remote(
            tab.at[1, slot, piece], tab.at[1, 2, piece], send_sem.at[0], y_sem.at[1], to
        ).start()

    ids_all = all_of(idb.at[pl.ds(0, others)], send_sem.at[1], recv_sem.at[1])
    ids_all.wait_recv()
    cols = idb[...].reshape(NX * NZ * PICKS, examples).T
    wide = [
        jnp.broadcast_to(cols[:, c : c + 1], (examples, 128)) for c in range(NX * NZ * PICKS)
    ]
    lane = lax.broadcasted_iota(jnp.int32, (examples, 128), 1)
    for ky in range(NY):
        for cut in range(0, rows, 128):
            here = lane + (peers_y[ky] * rows + cut)
            for d in range(NX * NZ):
                first = jnp.where(wide[PICKS * d] == here, 1.0, 0.0)
                count = jnp.where(wide[PICKS * d + 1] == here, first + 1.0, first)
                onehot[
                    d * examples : (d + 1) * examples, ky * rows + cut : ky * rows + cut + 128
                ] = count.astype(jnp.bfloat16)

    block = NZ * examples

    def partial(h, first):
        total = jnp.dot(
            onehot[first : first + block, :],
            tab[h].reshape(NY * rows, 128),
            preferred_element_type=jnp.float32,
        )
        return total.reshape(NZ, examples, 128)

    def swap(h, i):
        return remote(x_out.at[h, i], x_in.at[h, i], send_sem.at[3], x_sem.at[h, i], at(0, 0, 1))

    for h in range(2):
        all_of(tab.at[h, pl.ds(1, 3 - h)], send_sem.at[0], y_sem.at[h]).wait_recv()
        x_out[h] = partial(h, 0)
        for i in range(NZ - 1):
            swap(h, i).start()
        part[h] = partial(h, block)
    for h in range(2):
        swap(h, NZ - 1).start()

    sm_all = all_of(smb.at[0, pl.ds(0, others)], send_sem.at[2], recv_sem.at[2])
    sm_all.wait_recv()
    for k in (2, 1, 3):
        remote(
            smb.at[0], smb.at[NY - k], send_sem.at[4], recv_sem.at[4], peers_y[k]
        ).start()

    for h in range(2):
        for i, k in enumerate(FAR_FIRST[:-1]):
            swap(h, i).wait_recv()
            z_out[h, i] = part[h, i] + x_in[h, i]
            remote(
                z_out.at[h, i],
                z_in.at[h, FAR_FIRST.index(-k % NZ)],
                send_sem.at[5],
                recv_sem.at[5],
                at(k, 0, 0),
            ).start()

    sm_y = all_of(smb.at[pl.ds(1, NY - 1)], send_sem.at[4], recv_sem.at[4])
    sm_y.wait_recv()
    count = NY * NX * NZ * 2
    small = smb[...].reshape(count, 256)
    place = lax.broadcasted_iota(jnp.int32, (examples, count), 1)
    spot = lax.rem(place // 2, NX * NZ)
    sx = jnp.where(spot < NZ, 1 - x, x)
    sz = z
    for i, k in enumerate(FAR_FIRST):
        sz = jnp.where(lax.rem(spot, NZ) == i, lax.rem(z + k, NZ), sz)
    sy = lax.rem(place // (2 * NZ * NX) + y, NY)
    row = ((sz * NY + sy) * NX + sx) * 2 + lax.rem(place, 2)
    pick_cols = picks[...].reshape(2, examples).T
    found = [
        jnp.dot(
            jnp.where(pick_cols[:, i : i + 1] == row, 1.0, 0.0).astype(jnp.bfloat16),
            small,
            preferred_element_type=jnp.float32,
        )
        for i in range(2)
    ]
    scaled = dense[...] * found[1]

    for h in range(2):
        swap(h, NZ - 1).wait_recv()

    z_all = all_of(z_in, send_sem.at[5], recv_sem.at[5])
    z_all.wait_recv()
    totals = []
    for h in range(2):
        pooled = part[h, NZ - 1] + x_in[h, NZ - 1]
        for i in range(NZ - 1):
            pooled += z_in[h, i]
        cut = slice(h * 128, (h + 1) * 128)
        totals.append(scaled[:, cut] + pooled * PICKS ** (-0.5) * found[0][:, cut])
    square = totals[0] * totals[0] + totals[1] * totals[1]
    power = jnp.sum(square, axis=-1, keepdims=True) / 256.0
    inverse = lax.rsqrt(power + 1e-06)
    for h in range(2):
        out_ref[:, h * 128 : (h + 1) * 128] = totals[h] * inverse

    all_of(tab.at[:, pl.ds(1, 3)], send_sem.at[0], y_sem.at[0]).wait_send()
    ids_all.wait_send()
    sm_all.wait_send()
    all_of(x_out, send_sem.at[3], recv_sem.at[3]).wait_send()
    sm_y.wait_send()
    all_of(z_out, send_sem.at[5], recv_sem.at[5]).wait_send()


def shards(item_ids, large_table, dense_part, small_ids, small_table, scale_ids):
    examples, features = dense_part.shape
    rows = large_table.shape[0]
    any_space = pl.BlockSpec(memory_space=pl.ANY)
    dma = pltpu.SemaphoreType.DMA
    block = (examples, 128)
    return pl.pallas_call(
        kernel,
        out_shape=pltpu.VMEM((examples, features), jnp.float32),
        in_specs=[any_space] * 6,
        out_specs=pl.BlockSpec(memory_space=pltpu.VMEM),
        scratch_shapes=[
            pltpu.VMEM((2, NY, rows, 128), jnp.bfloat16),
            pltpu.VMEM((NX * NZ, PICKS, examples), jnp.int32),
            pltpu.VMEM((NY, NX * NZ, 2, features), jnp.bfloat16),
            pltpu.VMEM((examples, features), jnp.float32),
            pltpu.VMEM((2, 1, examples), jnp.int32),
            pltpu.VMEM((NX * NZ * examples, NY * rows), jnp.bfloat16),
            pltpu.VMEM((2, NZ, *block), jnp.float32),
            pltpu.VMEM((2, NZ, *block), jnp.float32),
            pltpu.VMEM((2, NZ, *block), jnp.float32),
            pltpu.VMEM((2, NZ - 1, *block), jnp.float32),
            pltpu.VMEM((2, NZ - 1, *block), jnp.float32),
            dma((7,)),
            dma((6,)),
            dma((6,)),
            dma((2, NZ)),
            dma((2,)),
            dma((2,)),
        ],
        compiler_params=pltpu.CompilerParams(collective_id=0, has_side_effects=True),
    )(
        item_ids.T,
        large_table,
        dense_part,
        small_ids.reshape(1, examples),
        scale_ids.reshape(1, examples),
        small_table,
    )


def solution(mesh):
    return jax.shard_map(
        shards,
        mesh=mesh,
        in_specs=(
            P(("ens", "bank"), None),
            P(("ens", "bank"), None),
            P(("ens", "bank"), None),
            P(("ens", "bank")),
            P(("ens", "bank"), None),
            P(("ens", "bank")),
        ),
        out_specs=P(("ens", "bank"), None),
        check_vma=False,
    )
```

time: 127 us -> 25.6 us (0.20)
  waiting for transfers between devices: 57.1 us -> 0 us
  starting transfers between devices: 29.9 us -> 0 us
  Pallas kernels: 0 us -> 24.9 us
  local copies, waits for them, and re-layouts: 23.4 us -> 0.62 us
  other arithmetic: 15.4 us -> 0 us
    all_to_all x3 -> x0, waiting for transfers between devices: 57.1 us -> none  [the longest x1 47.3 us: sum_at_owner(): lax.all_to_all(blocks, axis, split_axis=0, concat_axis=0, tiled=True)]
    all_to_all x3 -> x0, starting transfers between devices: 29.9 us -> none  [the longest x2 18.5 us: from_everyone(): lax.all_to_all(jnp.broadcast_to(value[None], (length, *value.shape)), axi...]
    pallas_call x0 -> x1, Pallas kernels: none -> 24.9 us  [shards(): pl.pallas_call(kernel, out_shape=pltpu.VMEM((examples, features), jnp.flo...]
    gather x4 -> x0, local copies, waits for them, and re-layouts: 18.1 us -> none  [the longest x2 16.8 us: local_rows(): jnp.take(table_part, jnp.clip(place, 0, table_part.shape[0] - 1), axis=0)]
    reduce_sum x3 -> x0, other arithmetic: 14.6 us -> none  [the longest x1 14.2 us: shards(): jnp.sum(local_rows(large_table, all_ids, big_first), axis=1)]
    broadcast_in_dim x2 -> x0, local copies, waits for them, and re-layouts: 2.67 us -> none  [from_everyone(): jnp.broadcast_to(value[None], (length, *value.shape))]
    and x2 -> x0, local copies, waits for them, and re-layouts: 1.43 us -> none  [the longest x1 0.96 us: local_rows(): inside = (place >= 0) & (place < table_part.shape[0])]
  transfers between devices with their start and end apart: 3 -> 0, of which waited for: 2 -> 0; matrix products, arithmetic and copies ran while one was open for 28% -> 0% of each run, Pallas kernels for 0% -> 0%
where the time goes in v2:
time: 25.6 us; the launch traced here: 25.5 us
  Pallas kernels  24.9 us (97%)
  local copies, waits for them, and re-layouts  0.62 us (2%)
    pallas_call x1, Pallas kernels, shards(): pl.pallas_call(kernel, out_shape=pltpu.VMEM((examples, features), jnp.flo...  24.9 us
    unnamed x1, local copies, waits for them, and re-layouts  0.62 us

profile of v2, /device:TPU:2, one launch (start us, length us, event | category | flops | bytes accessed | tf_op | source)
XLA Modules:
  0.0 25.5 jit_solution(16239624201914871353)
XLA Ops:
  0.0 24.9 %shard_map.64 = f32[32,256]{1,0:T(8,128)S(1)} custom-call(s32[2,32]{1,0:T(2,128)} %bitcast.3, bf16[256,256]{1,0:T(8,128)(2,1)} %table_hbm.1, f32[32,256]{1,0:T(8,128)} %dense_hbm.1, s32[1,32]{1,0:T(1,128)} %bitcast.4, s32[1,32]{1,0:T(1,128)} %bitcast.5, bf16[2,256]{1,0:T(2,128)(2,1)} %small_hbm.1), custom_call_target="tpu_custom_call" | custom-call | tf_op jit(solution)/shard_map/pallas_call | solution.py:236
  24.9 0.6 %copy.8 = f32[32,256]{1,0:T(8,128)} copy(f32[32,256]{1,0:T(8,128)S(1)} %shard_map.64) | data formatting | bytes 65536

commit v3 on v2

v3 whole, which is shorter than its diff:
```python
import functools

import jax
import jax.numpy as jnp
from jax import lax
from jax.experimental import pallas as pl
from jax.experimental.pallas import tpu as pltpu
from jax.sharding import PartitionSpec as P

PICKS = 2
NZ, NY, NX = 8, 4, 2
NEAR, COLUMN = 4, 16
OTHERS = COLUMN - 1
FAR_0 = (4, 5, 7, 6, 2, 3, 1, 0)
FAR_1 = (2, 3, 1, 0)
COLUMN_0 = [(f, k) for group in (FAR_0[:2], FAR_0[2:4], FAR_0[4:]) for f in (1, 0) for k in group]
COLUMN_1 = [
    pair
    for group in (FAR_1[:1], FAR_1[1:2], FAR_1[2:])
    for pair in [(f, k) for k in group for f in FAR_1[:-1]] + [(0, k) for k in group]
]
GROUPS = ((0, 4), (4, 4), (8, 8))
NEAREST = 2
MESH = pl.DeviceIdType.MESH


def kernel(
    ids_hbm,
    table_hbm,
    dense_hbm,
    small_ids_hbm,
    scale_ids_hbm,
    small_hbm,
    out_ref,
    tab,
    idb,
    smb,
    dense,
    picks,
    onehot,
    part,
    x_out,
    x_in,
    z_out,
    z_in,
    load_sem,
    send_sem,
    recv_sem,
    x_sem,
    y_sem,
    ids_sem,
):
    bank = lax.axis_index("bank")
    x = lax.rem(bank, NX)
    y = lax.rem(bank // NX, NY)
    z = bank // (NX * NY)
    second = lax.rem(lax.axis_index("ens"), 2) == 1

    def plan(first_core, second_core):
        return jnp.where(second, second_core, first_core)

    def flip(value, bit):
        return 1 - value if bit else value

    def change(value, bits):
        return sum(flip(lax.rem(value // b, 2), bits // b % 2) * b for b in (1, 2, 4))

    near = [
        plan(
            change(y, k) * NX,
            change(lax.rem(z, 2), k // 2) * (NY * NX) + change(x, k % 2 ^ k // 2),
        )
        for k in range(NEAR)
    ]

    def column_0(f, k):
        return change(x, f) + change(z, k) * (NY * NX)

    def column_1(f, k):
        return change(y, f) * NX + change(z // 2, k) * (2 * NY * NX)

    column = [plan(column_0(*COLUMN_0[i]), column_1(*COLUMN_1[i])) for i in range(COLUMN)]

    def remote(src, dst, send, recv, to):
        return pltpu.make_async_remote_copy(
            src_ref=src,
            dst_ref=dst,
            send_sem=send,
            recv_sem=recv,
            device_id={"bank": to},
            device_id_type=MESH,
        )

    rows = table_hbm.shape[0]
    examples = dense_hbm.shape[0]
    sharers = [near[k] + column[OTHERS] for k in range(NEAR)]
    askers = [near[0] + column[i] for i in range(OTHERS)]

    barrier = pltpu.get_barrier_semaphore()
    for to in sharers[1:] + askers:
        pl.semaphore_signal(barrier, inc=1, device_id={"bank": to}, device_id_type=MESH)

    loads = [
        pltpu.make_async_copy(table_hbm.at[:, pl.ds(0, 128)], tab.at[0, 0], load_sem.at[0]),
        pltpu.make_async_copy(table_hbm.at[:, pl.ds(128, 128)], tab.at[1, 0], load_sem.at[0]),
        pltpu.make_async_copy(ids_hbm, idb.at[OTHERS], load_sem.at[1]),
        pltpu.make_async_copy(small_hbm, smb.at[0, OTHERS], load_sem.at[2]),
        pltpu.make_async_copy(dense_hbm, dense, load_sem.at[3]),
        pltpu.make_async_copy(small_ids_hbm, picks.at[0], load_sem.at[4]),
        pltpu.make_async_copy(scale_ids_hbm, picks.at[1], load_sem.at[4]),
    ]
    for load in loads:
        load.start()
    for buf, i in (
        (tab.at[:, 0], 0), (idb.at[OTHERS], 1), (smb.at[0, OTHERS], 2), (dense, 3), (picks, 4)
    ):
        pltpu.make_async_copy(buf, buf, load_sem.at[i]).wait()
    pl.semaphore_wait(barrier, NEAR - 1 + OTHERS)

    for i in range(OTHERS):
        remote(
            idb.at[OTHERS],
            idb.at[i],
            send_sem.at[1],
            ids_sem.at[min(i // 4, NEAREST)],
            askers[i],
        ).start()
    for i in range(OTHERS):
        remote(
            smb.at[0, OTHERS],
            smb.at[0, i],
            send_sem.at[2],
            recv_sem.at[2],
            askers[i],
        ).start()
    for h in range(2):
        for k in (2, 1, 3):
            remote(
                tab.at[h, 0], tab.at[h, k], send_sem.at[0], y_sem.at[h], sharers[k]
            ).start()
    def all_of(ref, send, recv):
        return remote(ref, ref, send, recv, sharers[1])

    lane = lax.broadcasted_iota(jnp.int32, (examples, 128), 1)

    def mark_rows(group):
        first, blocks = GROUPS[group]
        arrived = idb.at[pl.ds(first, blocks - (group == NEAREST))]
        all_of(arrived, send_sem.at[1], ids_sem.at[group]).wait_recv()
        cols = idb[first : first + blocks].reshape(blocks * PICKS, examples).T
        wide = [
            jnp.broadcast_to(cols[:, c : c + 1], (examples, 128)) for c in range(blocks * PICKS)
        ]
        for k in range(NEAR):
            for cut in range(0, rows, 128):
                here = lane + (sharers[k] * rows + cut)
                for d in range(blocks):
                    once = jnp.where(wide[PICKS * d] == here, 1.0, 0.0)
                    count = jnp.where(wide[PICKS * d + 1] == here, once + 1.0, once)
                    onehot[
                        (first + d) * examples : (first + d + 1) * examples,
                        k * rows + cut : k * rows + cut + 128,
                    ] = count.astype(jnp.bfloat16)

    mark_rows(NEAREST)

    def partial(h, first, blocks):
        total = jnp.dot(
            onehot[first * examples : (first + blocks) * examples, :],
            tab[h].reshape(NEAR * rows, 128),
            preferred_element_type=jnp.float32,
        )
        return total.reshape(blocks, examples, 128)

    def wait_rows(h):
        all_of(tab.at[h, pl.ds(1, NEAR - 1)], send_sem.at[0], y_sem.at[h]).wait_recv()

    def by_core(steps):
        pl.when(jnp.logical_not(second))(functools.partial(steps, True))
        pl.when(second)(functools.partial(steps, False))

    def planes(first_core):
        return (len(FAR_0), 1) if first_core else (len(FAR_1), len(FAR_1) - 1)

    def first_peer(first_core, f):
        if first_core:
            return near[0] + column_0(1, 0)
        return near[0] + column_1(f, 0)

    def first_step(first_core):
        count, each = planes(first_core)
        width = count * each

        def send(h, i):
            k, j = i // each, i % each
            f = 1 if first_core else FAR_1[j]
            remote(
                x_out.at[h, i],
                x_in.at[h, i],
                send_sem.at[3],
                x_sem.at[h, k] if k < count - 1 else recv_sem.at[3],
                first_peer(first_core, f),
            ).start()

        def sums(h, group):
            first, blocks = GROUPS[group]
            k, planes_here = first * count // COLUMN, blocks * count // COLUMN
            outs = planes_here * each
            x_out[h, k * each : k * each + outs] = partial(h, first, outs)
            for i in range(k * each, min(k * each + outs, width - each)):
                send(h, i)

        def keep(h, group):
            first, blocks = GROUPS[group]
            k, planes_here = first * count // COLUMN, blocks * count // COLUMN
            part[h, k : k + planes_here] = partial(h, first + planes_here * each, planes_here)

        wait_rows(0)
        sums(0, NEAREST)
        for group in (1, 0):
            mark_rows(group)
            sums(0, group)
        wait_rows(1)
        for group in (2, 1, 0):
            sums(1, group)
        for h in range(2):
            for i in range(width - each, width):
                send(h, i)
        for group in (NEAREST, 1, 0):
            for h in range(2):
                keep(h, group)

    by_core(first_step)

    sm_all = all_of(smb.at[0, pl.ds(0, OTHERS)], send_sem.at[2], recv_sem.at[2])
    sm_all.wait_recv()
    for k in (2, 1, 3):
        remote(
            smb.at[0], smb.at[k], send_sem.at[4], recv_sem.at[4], sharers[k]
        ).start()

    def second_step(first_core):
        count, each = planes(first_core)
        half, quarter = count // 2, count // 4
        spans = ((0, quarter), (quarter, half), (half, count - 1))
        for h, group in [(0, 2), (0, 1), (0, 0)] + [(1, g) for g in (2, 1, 0)]:
            for k in range(*spans[group]):
                arrived = x_in.at[h, pl.ds(k * each, each)]
                all_of(arrived, send_sem.at[3], x_sem.at[h, k]).wait_recv()
                total = part[h, k]
                for j in range(each):
                    total += x_in[h, k * each + j]
                z_out[h, k] = total
                to = column_0(0, FAR_0[k]) if first_core else column_1(0, FAR_1[k])
                remote(
                    z_out.at[h, k],
                    z_in.at[h, k],
                    send_sem.at[5],
                    recv_sem.at[5],
                    near[0] + to,
                ).start()

    by_core(second_step)

    sm_y = all_of(smb.at[pl.ds(1, NEAR - 1)], send_sem.at[4], recv_sem.at[4])
    sm_y.wait_recv()
    count = NEAR * COLUMN * 2
    small = smb[...].reshape(count, 256)
    place = lax.broadcasted_iota(jnp.int32, (examples, count), 1)

    def chosen(values, index):
        result = values[0]
        for i in range(1, len(values)):
            result = jnp.where(index == i, values[i], result)
        return result

    holder = chosen(near, place // (2 * COLUMN)) + chosen(column, lax.rem(place // 2, COLUMN))
    row = holder * 2 + lax.rem(place, 2)
    pick_cols = picks[...].reshape(2, examples).T
    found = [
        jnp.dot(
            jnp.where(pick_cols[:, i : i + 1] == row, 1.0, 0.0).astype(jnp.bfloat16),
            small,
            preferred_element_type=jnp.float32,
        )
        for i in range(2)
    ]
    scaled = dense[...] * found[1]

    def collect(first_core):
        count, each = planes(first_core)
        own = pl.ds((count - 1) * each, each)
        all_of(x_in.at[:, own], send_sem.at[3], recv_sem.at[3]).wait_recv()
        all_of(z_in.at[:, pl.ds(0, count - 1)], send_sem.at[5], recv_sem.at[5]).wait_recv()
        for h in range(2):
            total = part[h, count - 1]
            for j in range(each):
                total += x_in[h, (count - 1) * each + j]
            for k in range(count - 1):
                total += z_in[h, k]
            part[h, 0] = total
        all_of(x_out.at[:, pl.ds(0, count * each)], send_sem.at[3], recv_sem.at[3]).wait_send()
        all_of(z_out.at[:, pl.ds(0, count - 1)], send_sem.at[5], recv_sem.at[5]).wait_send()

    by_core(collect)
    totals = []
    for h in range(2):
        pooled = part[h, 0]
        cut = slice(h * 128, (h + 1) * 128)
        totals.append(scaled[:, cut] + pooled * PICKS ** (-0.5) * found[0][:, cut])
    square = totals[0] * totals[0] + totals[1] * totals[1]
    power = jnp.sum(square, axis=-1, keepdims=True) / 256.0
    inverse = lax.rsqrt(power + 1e-06)
    for h in range(2):
        out_ref[:, h * 128 : (h + 1) * 128] = totals[h] * inverse

    all_of(tab.at[:, pl.ds(1, 3)], send_sem.at[0], y_sem.at[0]).wait_send()
    all_of(idb.at[pl.ds(0, OTHERS)], send_sem.at[1], recv_sem.at[1]).wait_send()
    sm_all.wait_send()
    sm_y.wait_send()


def shards(item_ids, large_table, dense_part, small_ids, small_table, scale_ids):
    examples, features = dense_part.shape
    rows = large_table.shape[0]
    any_space = pl.BlockSpec(memory_space=pl.ANY)
    dma = pltpu.SemaphoreType.DMA
    block = (examples, 128)
    return pl.pallas_call(
        kernel,
        out_shape=pltpu.VMEM((examples, features), jnp.float32),
        in_specs=[any_space] * 6,
        out_specs=pl.BlockSpec(memory_space=pltpu.VMEM),
        scratch_shapes=[
            pltpu.VMEM((2, NEAR, rows, 128), jnp.bfloat16),
            pltpu.VMEM((COLUMN, PICKS, examples), jnp.int32),
            pltpu.VMEM((NEAR, COLUMN, 2, features), jnp.bfloat16),
            pltpu.VMEM((examples, features), jnp.float32),
            pltpu.VMEM((2, 1, examples), jnp.int32),
            pltpu.VMEM((COLUMN * examples, NEAR * rows), jnp.bfloat16),
            pltpu.VMEM((2, 8, *block), jnp.float32),
            pltpu.VMEM((2, 12, *block), jnp.float32),
            pltpu.VMEM((2, 12, *block), jnp.float32),
            pltpu.VMEM((2, 7, *block), jnp.float32),
            pltpu.VMEM((2, 7, *block), jnp.float32),
            dma((5,)),
            dma((6,)),
            dma((6,)),
            dma((2, 7)),
            dma((2,)),
            dma((len(GROUPS),)),
        ],
        compiler_params=pltpu.CompilerParams(collective_id=0, has_side_effects=True),
    )(
        item_ids.T,
        large_table,
        dense_part,
        small_ids.reshape(1, examples),
        scale_ids.reshape(1, examples),
        small_table,
    )


def solution(mesh):
    return jax.shard_map(
        shards,
        mesh=mesh,
        in_specs=(
            P(("ens", "bank"), None),
            P(("ens", "bank"), None),
            P(("ens", "bank"), None),
            P(("ens", "bank")),
            P(("ens", "bank"), None),
            P(("ens", "bank")),
        ),
        out_specs=P(("ens", "bank"), None),
        check_vma=False,
    )
```

time: 25.6 us -> 24.6 us (0.961)
  Pallas kernels: 24.9 us -> 23.8 us
    pallas_call x1, Pallas kernels: 24.9 us -> 23.8 us  [shards(): pl.pallas_call(kernel, out_shape=pltpu.VMEM((examples, features), jnp.flo...]
where the time goes in v3:
time: 24.6 us; the launch traced here: 24.5 us
  Pallas kernels  23.8 us (97%)
  local copies, waits for them, and re-layouts  0.62 us (3%)
    pallas_call x1, Pallas kernels, shards(): pl.pallas_call(kernel, out_shape=pltpu.VMEM((examples, features), jnp.flo...  23.8 us
    unnamed x1, local copies, waits for them, and re-layouts  0.62 us

profile of v3, /device:TPU:2, one launch (start us, length us, event | category | flops | bytes accessed | tf_op | source)
XLA Modules:
  0.0 24.5 jit_solution(6103854045861239818)
XLA Ops:
  0.0 23.8 %shard_map.64 = f32[32,256]{1,0:T(8,128)S(1)} custom-call(s32[2,32]{1,0:T(2,128)} %bitcast.3, bf16[256,256]{1,0:T(8,128)(2,1)} %table_hbm.1, f32[32,256]{1,0:T(8,128)} %dense_hbm.1, s32[1,32]{1,0:T(1,128)} %bitcast.4, s32[1,32]{1,0:T(1,128)} %bitcast.5, bf16[2,256]{1,0:T(2,128)(2,1)} %small_hbm.1), custom_call_target="tpu_custom_call" | custom-call | tf_op jit(solution)/shard_map/pallas_call | solution.py:329
  23.8 0.6 %copy.8 = f32[32,256]{1,0:T(8,128)} copy(f32[32,256]{1,0:T(8,128)S(1)} %shard_map.64) | data formatting | bytes 65536

commit v4 on v3

--- a/solution.py
+++ b/solution.py
@@ -182,6 +182,13 @@
     def planes(first_core):
         return (len(FAR_0), 1) if first_core else (len(FAR_1), len(FAR_1) - 1)
 
+    def in_order(first_core, steps):
+        if not first_core:
+            return steps((2, 1, 0))
+        late = z >= NZ // 2
+        pl.when(late)(functools.partial(steps, (0, 1, 2)))
+        pl.when(jnp.logical_not(late))(functools.partial(steps, (2, 1, 0)))
+
     def first_peer(first_core, f):
         if first_core:
             return near[0] + column_0(1, 0)
@@ -221,8 +228,12 @@
             mark_rows(group)
             sums(0, group)
         wait_rows(1)
-        for group in (2, 1, 0):
-            sums(1, group)
+
+        def second_half(order):
+            for group in order:
+                sums(1, group)
+
+        in_order(first_core, second_half)
         for h in range(2):
             for i in range(width - each, width):
                 send(h, i)
@@ -243,8 +254,9 @@
         count, each = planes(first_core)
         half, quarter = count // 2, count // 4
         spans = ((0, quarter), (quarter, half), (half, count - 1))
-        for h, group in [(0, 2), (0, 1), (0, 0)] + [(1, g) for g in (2, 1, 0)]:
-            for k in range(*spans[group]):
+
+        def pass_on(h, order):
+            for k in [k for group in order for k in range(*spans[group])]:
                 arrived = x_in.at[h, pl.ds(k * each, each)]
                 all_of(arrived, send_sem.at[3], x_sem.at[h, k]).wait_recv()
                 total = part[h, k]
@@ -259,6 +271,9 @@
                     recv_sem.at[5],
                     near[0] + to,
                 ).start()
+
+        pass_on(0, (2, 1, 0))
+        in_order(first_core, functools.partial(pass_on, 1))
 
     by_core(second_step)
 

time: 24.6 us -> 24.5 us (level)
  no operation moved by 1% of the time
where the time goes in v4:
time: 24.5 us; the launch traced here: 24.2 us
  Pallas kernels  23.6 us (96%)
  local copies, waits for them, and re-layouts  0.62 us (3%)
    pallas_call x1, Pallas kernels, shards(): pl.pallas_call(kernel, out_shape=pltpu.VMEM((examples, features), jnp.flo...  23.6 us
    unnamed x1, local copies, waits for them, and re-layouts  0.62 us

profile of v4, /device:TPU:2, one launch (start us, length us, event | category | flops | bytes accessed | tf_op | source)
XLA Modules:
  0.0 24.2 jit_solution(9194046001059087126)
XLA Ops:
  0.0 23.6 %shard_map.64 = f32[32,256]{1,0:T(8,128)S(1)} custom-call(s32[2,32]{1,0:T(2,128)} %bitcast.3, bf16[256,256]{1,0:T(8,128)(2,1)} %table_hbm.1, f32[32,256]{1,0:T(8,128)} %dense_hbm.1, s32[1,32]{1,0:T(1,128)} %bitcast.4, s32[1,32]{1,0:T(1,128)} %bitcast.5, bf16[2,256]{1,0:T(2,128)(2,1)} %small_hbm.1), custom_call_target="tpu_custom_call" | custom-call | tf_op jit(solution)/shard_map/pallas_call | solution.py:344
  23.6 0.6 %copy.8 = f32[32,256]{1,0:T(8,128)} copy(f32[32,256]{1,0:T(8,128)S(1)} %shard_map.64) | data formatting | bytes 65536

commit v5 on v4

--- a/solution.py
+++ b/solution.py
@@ -11,7 +11,7 @@
 NZ, NY, NX = 8, 4, 2
 NEAR, COLUMN = 4, 16
 OTHERS = COLUMN - 1
-FAR_0 = (4, 5, 7, 6, 2, 3, 1, 0)
+FAR_0 = (4, 5, 7, 6, 3, 2, 1, 0)
 FAR_1 = (2, 3, 1, 0)
 COLUMN_0 = [(f, k) for group in (FAR_0[:2], FAR_0[2:4], FAR_0[4:]) for f in (1, 0) for k in group]
 COLUMN_1 = [
@@ -43,8 +43,7 @@
     x_in,
     z_out,
     z_in,
-    load_sem,
-    send_sem,
+    here_sem,
     recv_sem,
     x_sem,
     y_sem,
@@ -101,27 +100,27 @@
         pl.semaphore_signal(barrier, inc=1, device_id={"bank": to}, device_id_type=MESH)
 
     loads = [
-        pltpu.make_async_copy(table_hbm.at[:, pl.ds(0, 128)], tab.at[0, 0], load_sem.at[0]),
-        pltpu.make_async_copy(table_hbm.at[:, pl.ds(128, 128)], tab.at[1, 0], load_sem.at[0]),
-        pltpu.make_async_copy(ids_hbm, idb.at[OTHERS], load_sem.at[1]),
-        pltpu.make_async_copy(small_hbm, smb.at[0, OTHERS], load_sem.at[2]),
-        pltpu.make_async_copy(dense_hbm, dense, load_sem.at[3]),
-        pltpu.make_async_copy(small_ids_hbm, picks.at[0], load_sem.at[4]),
-        pltpu.make_async_copy(scale_ids_hbm, picks.at[1], load_sem.at[4]),
+        pltpu.make_async_copy(table_hbm.at[:, pl.ds(0, 128)], tab.at[0, 0], here_sem.at[0]),
+        pltpu.make_async_copy(table_hbm.at[:, pl.ds(128, 128)], tab.at[1, 0], here_sem.at[0]),
+        pltpu.make_async_copy(ids_hbm, idb.at[OTHERS], here_sem.at[1]),
+        pltpu.make_async_copy(small_hbm, smb.at[0, OTHERS], here_sem.at[2]),
+        pltpu.make_async_copy(dense_hbm, dense, here_sem.at[3]),
+        pltpu.make_async_copy(small_ids_hbm, picks.at[0], here_sem.at[4]),
+        pltpu.make_async_copy(scale_ids_hbm, picks.at[1], here_sem.at[4]),
     ]
     for load in loads:
         load.start()
     for buf, i in (
         (tab.at[:, 0], 0), (idb.at[OTHERS], 1), (smb.at[0, OTHERS], 2), (dense, 3), (picks, 4)
     ):
-        pltpu.make_async_copy(buf, buf, load_sem.at[i]).wait()
+        pltpu.make_async_copy(buf, buf, here_sem.at[i]).wait()
     pl.semaphore_wait(barrier, NEAR - 1 + OTHERS)
 
     for i in range(OTHERS):
         remote(
             idb.at[OTHERS],
             idb.at[i],
-            send_sem.at[1],
+            here_sem.at[1],
             ids_sem.at[min(i // 4, NEAREST)],
             askers[i],
         ).start()
@@ -129,14 +128,14 @@
         remote(
             smb.at[0, OTHERS],
             smb.at[0, i],
-            send_sem.at[2],
+            here_sem.at[2],
             recv_sem.at[2],
             askers[i],
         ).start()
     for h in range(2):
         for k in (2, 1, 3):
             remote(
-                tab.at[h, 0], tab.at[h, k], send_sem.at[0], y_sem.at[h], sharers[k]
+                tab.at[h, 0], tab.at[h, k], here_sem.at[0], y_sem.at[h], sharers[k]
             ).start()
     def all_of(ref, send, recv):
         return remote(ref, ref, send, recv, sharers[1])
@@ -146,7 +145,7 @@
     def mark_rows(group):
         first, blocks = GROUPS[group]
         arrived = idb.at[pl.ds(first, blocks - (group == NEAREST))]
-        all_of(arrived, send_sem.at[1], ids_sem.at[group]).wait_recv()
+        all_of(arrived, here_sem.at[1], ids_sem.at[group]).wait_recv()
         cols = idb[first : first + blocks].reshape(blocks * PICKS, examples).T
         wide = [
             jnp.broadcast_to(cols[:, c : c + 1], (examples, 128)) for c in range(blocks * PICKS)
@@ -173,7 +172,7 @@
         return total.reshape(blocks, examples, 128)
 
     def wait_rows(h):
-        all_of(tab.at[h, pl.ds(1, NEAR - 1)], send_sem.at[0], y_sem.at[h]).wait_recv()
+        all_of(tab.at[h, pl.ds(1, NEAR - 1)], here_sem.at[0], y_sem.at[h]).wait_recv()
 
     def by_core(steps):
         pl.when(jnp.logical_not(second))(functools.partial(steps, True))
@@ -204,7 +203,7 @@
             remote(
                 x_out.at[h, i],
                 x_in.at[h, i],
-                send_sem.at[3],
+                here_sem.at[3],
                 x_sem.at[h, k] if k < count - 1 else recv_sem.at[3],
                 first_peer(first_core, f),
             ).start()
@@ -243,11 +242,11 @@
 
     by_core(first_step)
 
-    sm_all = all_of(smb.at[0, pl.ds(0, OTHERS)], send_sem.at[2], recv_sem.at[2])
+    sm_all = all_of(smb.at[0, pl.ds(0, OTHERS)], here_sem.at[2], recv_sem.at[2])
     sm_all.wait_recv()
     for k in (2, 1, 3):
         remote(
-            smb.at[0], smb.at[k], send_sem.at[4], recv_sem.at[4], sharers[k]
+            smb.at[0], smb.at[k], here_sem.at[4], recv_sem.at[4], sharers[k]
         ).start()
 
     def second_step(first_core):
@@ -258,7 +257,7 @@
         def pass_on(h, order):
             for k in [k for group in order for k in range(*spans[group])]:
                 arrived = x_in.at[h, pl.ds(k * each, each)]
-                all_of(arrived, send_sem.at[3], x_sem.at[h, k]).wait_recv()
+                all_of(arrived, here_sem.at[3], x_sem.at[h, k]).wait_recv()
                 total = part[h, k]
                 for j in range(each):
                     total += x_in[h, k * each + j]
@@ -267,7 +266,7 @@
                 remote(
                     z_out.at[h, k],
                     z_in.at[h, k],
-                    send_sem.at[5],
+                    here_sem.at[5],
                     recv_sem.at[5],
                     near[0] + to,
                 ).start()
@@ -277,7 +276,7 @@
 
     by_core(second_step)
 
-    sm_y = all_of(smb.at[pl.ds(1, NEAR - 1)], send_sem.at[4], recv_sem.at[4])
+    sm_y = all_of(smb.at[pl.ds(1, NEAR - 1)], here_sem.at[4], recv_sem.at[4])
     sm_y.wait_recv()
     count = NEAR * COLUMN * 2
     small = smb[...].reshape(count, 256)
@@ -305,8 +304,8 @@
     def collect(first_core):
         count, each = planes(first_core)
         own = pl.ds((count - 1) * each, each)
-        all_of(x_in.at[:, own], send_sem.at[3], recv_sem.at[3]).wait_recv()
-        all_of(z_in.at[:, pl.ds(0, count - 1)], send_sem.at[5], recv_sem.at[5]).wait_recv()
+        all_of(x_in.at[:, own], here_sem.at[3], recv_sem.at[3]).wait_recv()
+        all_of(z_in.at[:, pl.ds(0, count - 1)], here_sem.at[5], recv_sem.at[5]).wait_recv()
         for h in range(2):
             total = part[h, count - 1]
             for j in range(each):
@@ -314,8 +313,8 @@
             for k in range(count - 1):
                 total += z_in[h, k]
             part[h, 0] = total
-        all_of(x_out.at[:, pl.ds(0, count * each)], send_sem.at[3], recv_sem.at[3]).wait_send()
-        all_of(z_out.at[:, pl.ds(0, count - 1)], send_sem.at[5], recv_sem.at[5]).wait_send()
+        all_of(x_out.at[:, pl.ds(0, count * each)], here_sem.at[3], recv_sem.at[3]).wait_send()
+        all_of(z_out.at[:, pl.ds(0, count - 1)], here_sem.at[5], recv_sem.at[5]).wait_send()
 
     by_core(collect)
     totals = []
@@ -329,8 +328,8 @@
     for h in range(2):
         out_ref[:, h * 128 : (h + 1) * 128] = totals[h] * inverse
 
-    all_of(tab.at[:, pl.ds(1, 3)], send_sem.at[0], y_sem.at[0]).wait_send()
-    all_of(idb.at[pl.ds(0, OTHERS)], send_sem.at[1], recv_sem.at[1]).wait_send()
+    all_of(tab.at[:, pl.ds(1, 3)], here_sem.at[0], y_sem.at[0]).wait_send()
+    all_of(idb.at[pl.ds(0, OTHERS)], here_sem.at[1], recv_sem.at[1]).wait_send()
     sm_all.wait_send()
     sm_y.wait_send()
 
@@ -358,7 +357,6 @@
             pltpu.VMEM((2, 12, *block), jnp.float32),
             pltpu.VMEM((2, 7, *block), jnp.float32),
             pltpu.VMEM((2, 7, *block), jnp.float32),
-            dma((5,)),
             dma((6,)),
             dma((6,)),
             dma((2, 7)),

time: 24.5 us -> 24.3 us (level)
  no operation moved by 1% of the time
where the time goes in v5:
time: 24.3 us; the launch traced here: 24.2 us
  Pallas kernels  23.6 us (97%)
  local copies, waits for them, and re-layouts  0.62 us (3%)
    pallas_call x1, Pallas kernels, shards(): pl.pallas_call(kernel, out_shape=pltpu.VMEM((examples, features), jnp.flo...  23.6 us
    unnamed x1, local copies, waits for them, and re-layouts  0.62 us

profile of v5, /device:TPU:2, one launch (start us, length us, event | category | flops | bytes accessed | tf_op | source)
XLA Modules:
  0.0 24.2 jit_solution(3407442771932545958)
XLA Ops:
  0.0 23.6 %shard_map.64 = f32[32,256]{1,0:T(8,128)S(1)} custom-call(s32[2,32]{1,0:T(2,128)} %bitcast.3, bf16[256,256]{1,0:T(8,128)(2,1)} %table_hbm.1, f32[32,256]{1,0:T(8,128)} %dense_hbm.1, s32[1,32]{1,0:T(1,128)} %bitcast.4, s32[1,32]{1,0:T(1,128)} %bitcast.5, bf16[2,256]{1,0:T(2,128)(2,1)} %small_hbm.1), custom_call_target="tpu_custom_call" | custom-call | tf_op jit(solution)/shard_map/pallas_call | solution.py:343
  23.6 0.6 %copy.8 = f32[32,256]{1,0:T(8,128)} copy(f32[32,256]{1,0:T(8,128)S(1)} %shard_map.64) | data formatting | bytes 65536

commit v6 on v5

--- a/solution.py
+++ b/solution.py
@@ -96,7 +96,7 @@
     askers = [near[0] + column[i] for i in range(OTHERS)]
 
     barrier = pltpu.get_barrier_semaphore()
-    for to in sharers[1:] + askers:
+    for to in askers + sharers[1:]:
         pl.semaphore_signal(barrier, inc=1, device_id={"bank": to}, device_id_type=MESH)
 
     loads = [
@@ -197,6 +197,9 @@
         count, each = planes(first_core)
         width = count * each
 
+        def group_of(k):
+            return min(k * COLUMN // count // 4, NEAREST)
+
         def send(h, i):
             k, j = i // each, i % each
             f = 1 if first_core else FAR_1[j]
@@ -204,7 +207,7 @@
                 x_out.at[h, i],
                 x_in.at[h, i],
                 here_sem.at[3],
-                x_sem.at[h, k] if k < count - 1 else recv_sem.at[3],
+                x_sem.at[h, group_of(k)] if k < count - 1 else recv_sem.at[3],
                 first_peer(first_core, f),
             ).start()
 
@@ -255,21 +258,26 @@
         spans = ((0, quarter), (quarter, half), (half, count - 1))
 
         def pass_on(h, order):
-            for k in [k for group in order for k in range(*spans[group])]:
-                arrived = x_in.at[h, pl.ds(k * each, each)]
-                all_of(arrived, here_sem.at[3], x_sem.at[h, k]).wait_recv()
-                total = part[h, k]
-                for j in range(each):
-                    total += x_in[h, k * each + j]
-                z_out[h, k] = total
-                to = column_0(0, FAR_0[k]) if first_core else column_1(0, FAR_1[k])
-                remote(
-                    z_out.at[h, k],
-                    z_in.at[h, k],
-                    here_sem.at[5],
-                    recv_sem.at[5],
-                    near[0] + to,
-                ).start()
+            for group in order:
+                first, last = spans[group]
+                arrived = x_in.at[h, pl.ds(first * each, (last - first) * each)]
+                all_of(arrived, here_sem.at[3], x_sem.at[h, group]).wait_recv()
+                for k in range(first, last):
+                    pass_block(h, k)
+
+        def pass_block(h, k):
+            total = part[h, k]
+            for j in range(each):
+                total += x_in[h, k * each + j]
+            z_out[h, k] = total
+            to = column_0(0, FAR_0[k]) if first_core else column_1(0, FAR_1[k])
+            remote(
+                z_out.at[h, k],
+                z_in.at[h, k],
+                here_sem.at[5],
+                recv_sem.at[5],
+                near[0] + to,
+            ).start()
 
         pass_on(0, (2, 1, 0))
         in_order(first_core, functools.partial(pass_on, 1))
@@ -359,7 +367,7 @@
             pltpu.VMEM((2, 7, *block), jnp.float32),
             dma((6,)),
             dma((6,)),
-            dma((2, 7)),
+            dma((2, len(GROUPS))),
             dma((2,)),
             dma((len(GROUPS),)),
         ],

time: 24.3 us -> 24.4 us (level)
  no operation moved by 1% of the time
where the time goes in v6:
time: 24.4 us; the launch traced here: 24.3 us
  Pallas kernels  23.6 us (97%)
  local copies, waits for them, and re-layouts  0.62 us (3%)
    pallas_call x1, Pallas kernels, shards(): pl.pallas_call(kernel, out_shape=pltpu.VMEM((examples, features), jnp.flo...  23.6 us
    unnamed x1, local copies, waits for them, and re-layouts  0.62 us

profile of v6, /device:TPU:2, one launch (start us, length us, event | category | flops | bytes accessed | tf_op | source)
XLA Modules:
  0.0 24.3 jit_solution(3324270718679117452)
XLA Ops:
  0.0 23.6 %shard_map.64 = f32[32,256]{1,0:T(8,128)S(1)} custom-call(s32[2,32]{1,0:T(2,128)} %bitcast.3, bf16[256,256]{1,0:T(8,128)(2,1)} %table_hbm.1, f32[32,256]{1,0:T(8,128)} %dense_hbm.1, s32[1,32]{1,0:T(1,128)} %bitcast.4, s32[1,32]{1,0:T(1,128)} %bitcast.5, bf16[2,256]{1,0:T(2,128)(2,1)} %small_hbm.1), custom_call_target="tpu_custom_call" | custom-call | tf_op jit(solution)/shard_map/pallas_call | solution.py:351
  23.7 0.6 %copy.8 = f32[32,256]{1,0:T(8,128)} copy(f32[32,256]{1,0:T(8,128)S(1)} %shard_map.64) | data formatting | bytes 65536
